TPU v7x, 32 devices: a whole 2x2x4 slice. The times are simulated.
32 devices in a mesh: curve: 4 (over y, core), group: 8 (over z, x).
Axes of the slice: x: 2, y: 2, z: 4, core: 2. Of those that a mesh axis runs over, the one named last changes fastest.
Arguments:
- right_side: float32 [125, 16384], P(None, ('curve', 'group')), may hold values from -6 to 6, as said below
- conductivity: float32 [16384], P(('curve', 'group')), may hold values from 0.3 to 3
- destination: int32 [16384], P(('curve', 'group')), may hold values from 0 to 16383, as said below
- neighbour: int32 [6, 16384], P(None, ('curve', 'group')), may hold values from -1 to 1023, as said below
- orientation: int32 [6, 16384], P(None, ('curve', 'group')), may hold values from 0 to 3, as said below
- send_list: int32 [2, 8192], P(None, ('curve', 'group')), may hold values from 0 to 511, as said below
Outputs:
- solution: float32 [125, 16384], P(None, ('curve', 'group'))
- residual: float32 [125, 16384], P(None, ('curve', 'group'))
Inputs may be any that keep to these rules, and one draw needn't show every extreme that they name: `right_side`: custom normal-like values. `destination`: A permutation of all cells. Devices are ordered along the curve with curve slowest; every cell's new device is its old device or the one just before or after it. From each device at most 64 cells go to the next device and exactly as many come back from it; 64 is reached at some pair of neighbouring devices in every draw. `neighbour`: values below 512 are local cells of the same device. Only face 0 may name a slot from 512 to 512 + 256 - 1 (filled by the previous device from its send_list row 1), only face 1 a slot from 768 up (filled by the next device from its send_list row 0). Faces are paired: the cell across face f sees this cell across face f xor 1. -1 only at the domain boundary; the first device has no partner across its face 0 slots and the last none across face 1 slots. `orientation`: both sides of a shared face carry the same code; ignored where neighbour is -1. `send_list`: per device 256 distinct local cells in each row.
All inputs are finite; a program needn't handle non-finite values.
Results may differ from a plain program's by a relative error of at most 0.00015.
Values sent between devices are 32-bit elements; how exact they have to be, the bound alone decides.
No kernel may reach another device: no remote copies, remote signals or barrier semaphores. Data moves between devices by JAX's collectives and lax.ppermute only.
A program may use at most 64 MiB of HBM per device.

v0:
```python
import functools

import jax
import jax.numpy as jnp
import numpy as np
from jax import lax
from jax.experimental import pallas as pl
from jax.experimental.pallas import tpu as pltpu
from jax.sharding import PartitionSpec as P


NODES = 5
FACE = NODES * NODES
BLOCK = NODES**3
MOVE = 64
LANES = 128
ROWS = 128
HALF = 32
SLAB = 2 * HALF
FACES = 6
PENALTY = 80.0
AXES = ("curve", "group")
VMEM_LIMIT = 24 * 1024 * 1024

GAUSS_POINTS = (-0.906179845938664, -0.5384693101056831, 0.0, 0.5384693101056831, 0.906179845938664)
GAUSS_WEIGHTS = (
    0.2369268850561891,
    0.4786286704993665,
    0.5688888888888889,
    0.4786286704993665,
    0.2369268850561891,
)


def lagrange_value(points, position, location):
    value = 1.0
    for other in range(len(points)):
        if other != position:
            value = value * (location - points[other]) / (points[position] - points[other])
    return value


def lagrange_slope(points, position, location):
    total = 0.0
    for skipped in range(len(points)):
        if skipped == position:
            continue
        addend = 1.0 / (points[position] - points[skipped])
        for other in range(len(points)):
            if other != position and other != skipped:
                addend = addend * (location - points[other]) / (points[position] - points[other])
        total = total + addend
    return total


def basis_tables():
    points = [0.5 * (value + 1.0) for value in GAUSS_POINTS]
    weights = [0.5 * value for value in GAUSS_WEIGHTS]
    count = len(points)
    slopes = [[lagrange_slope(points, p, points[q]) for p in range(count)] for q in range(count)]
    start_value = [lagrange_value(points, p, 0.0) for p in range(count)]
    end_value = [lagrange_value(points, p, 1.0) for p in range(count)]
    start_slope = [-lagrange_slope(points, p, 0.0) for p in range(count)]
    end_slope = [lagrange_slope(points, p, 1.0) for p in range(count)]
    listed = (weights, slopes, start_value, end_value, start_slope, end_slope)
    return [np.asarray(np.asarray(table, np.float32), np.float64) for table in listed]


def along_axis(matrix, axis_id):
    factors = [np.eye(NODES)] * 3
    factors[axis_id] = matrix
    return np.kron(factors[0], np.kron(factors[1], factors[2]))


def parity_basis():
    root = np.sqrt(0.5)
    line = np.zeros((NODES, NODES))
    line[0, 0] = line[0, 4] = line[1, 1] = line[1, 3] = root
    line[2, 2] = 1.0
    line[3, 0], line[3, 4] = root, -root
    line[4, 1], line[4, 3] = root, -root
    odd = np.array([0, 0, 0, 1, 1])
    return np.kron(line, line), np.repeat(odd, NODES), np.tile(odd, NODES)


def split_two(matrix):
    high = matrix.astype(np.float32).astype(jnp.bfloat16)
    low = (matrix - high.astype(np.float64)).astype(np.float32).astype(jnp.bfloat16)
    return high, low


@functools.cache
def operator_constants():
    weights, slopes, *ends = basis_tables()
    cell_weight = np.kron(weights, np.kron(weights, weights))
    face_weight = np.kron(weights, weights)
    parity, odd_first, odd_second = parity_basis()
    stiff = np.zeros((BLOCK, BLOCK))
    for axis_id in range(3):
        grad = along_axis(slopes, axis_id)
        stiff += grad.T @ (cell_weight[:, None] * grad)
    trace = np.zeros((FACES * SLAB + ROWS, ROWS))
    back = np.zeros((ROWS, FACES * SLAB))
    for face in range(FACES):
        tangent = along_axis(ends[face % 2][None, :], face // 2)
        normal = along_axis(ends[2 + face % 2][None, :], face // 2)
        start = face * SLAB
        trace[start : start + FACE, :BLOCK] = parity @ tangent
        trace[start + HALF : start + HALF + FACE, :BLOCK] = parity @ normal
        spread = (face_weight[:, None] * parity.T)
        back[:BLOCK, start : start + FACE] = tangent.T @ spread
        back[:BLOCK, start + HALF : start + HALF + FACE] = -0.5 * normal.T @ spread
    trace[FACES * SLAB : FACES * SLAB + BLOCK, :BLOCK] = stiff
    high, low = split_two(trace)
    trace3 = np.concatenate([high, high, low], 1)
    trace_pair, trace_rest = trace3[: 2 * SLAB], trace3[2 * SLAB :]
    backs = []
    for first, last in ((0, 2), (2, FACES)):
        high, low = split_two(back[:, first * SLAB : last * SLAB])
        backs.append(np.concatenate([high, high, low], 1))
    weight_rows = np.zeros((ROWS, 1), np.float32)
    weight_rows[:BLOCK, 0] = cell_weight
    flips = np.zeros((SLAB, LANES), np.float32)
    for start in (0, HALF):
        flips[start : start + FACE, 0] = odd_first
        flips[start : start + FACE, 1] = odd_second
        flips[start : start + FACE, 2] = np.diag(parity @ (face_weight[:, None] * parity.T))
    return trace_pair, trace_rest, backs[0], backs[1], weight_rows, flips


def as_bf16(value):
    return value.astype(jnp.bfloat16)


def as_f32(value):
    return value.astype(jnp.float32)


def parts_of(value, count):
    pieces = []
    for step in range(count):
        piece = as_bf16(value)
        pieces.append(piece)
        if step + 1 < count:
            value = value - as_f32(piece)
    return pieces


def dot(left, right):
    return lax.dot_general(left, right, (((1,), (0,)), ((), ())), preferred_element_type=jnp.float32)


def dot_rows(left, right):
    return lax.dot_general(left, right, (((1,), (1,)), ((), ())), preferred_element_type=jnp.float32)


def times3(table3, value):
    high, low = parts_of(value, 2)
    return dot(table3, jnp.concatenate([high, low, high], 0))


def pick(value, chosen, count):
    rows = value.shape[0]
    out = dot(jnp.concatenate(parts_of(value, count), 0), chosen)
    total = out[(count - 1) * rows :]
    for step in reversed(range(count - 1)):
        total = total + out[step * rows : (step + 1) * rows]
    return total


def one_hot(index_row, rows, offset=0):
    ids = lax.broadcasted_iota(jnp.int32, (rows, index_row.shape[1]), 0)
    return as_bf16(jnp.where(ids == index_row - offset, 1.0, 0.0))


def call(kernel, outs, args, flops, scratch=(), far=0, out=pltpu.VMEM):
    moved = sum(a.size * a.dtype.itemsize for a in args) + sum(o.size * o.dtype.itemsize for o in outs)
    spaces = [pltpu.MemorySpace.HBM] * far + [pltpu.VMEM] * (len(args) - far)
    args = [pltpu.with_memory_space_constraint(a, pltpu.MemorySpace.HBM) if i < far else a
            for i, a in enumerate(args)]
    return pl.pallas_call(
        kernel,
        out_shape=list(outs),
        in_specs=[pl.BlockSpec(memory_space=space) for space in spaces],
        out_specs=[pl.BlockSpec(memory_space=out) for _ in outs],
        scratch_shapes=list(scratch),
        compiler_params=pltpu.CompilerParams(vmem_limit_bytes=VMEM_LIMIT),
        cost_estimate=pl.CostEstimate(flops=flops, bytes_accessed=moved, transcendentals=0),
    )(*args)


def f32(*shape):
    return jax.ShapeDtypeStruct(shape, jnp.float32)


def my_rank():
    return lax.axis_index("curve") * lax.axis_size("group") + lax.axis_index("group")


def pack_kernel(rhs_hbm, cond_hbm, dest_hbm, send_hbm, trace_hbm, nbr_hbm, near_up_ref, near_down_ref, far_up_ref,
                far_down_ref, packed_ref, payload_ref, stay_ref, send, nbr, trace, rhs, cond, dest_row, sems):
    cells = dest_row.shape[1]
    tiles = cells // LANES
    copies = [
        pltpu.make_async_copy(source, target, sems.at[place])
        for place, (source, target) in enumerate(
            ((dest_hbm, dest_row), (send_hbm, send), (cond_hbm, cond), (rhs_hbm, rhs), (trace_hbm, trace),
             (nbr_hbm, nbr))
        )
    ]
    for copy in copies:
        copy.start()
    copies[0].wait()
    copies[1].wait()
    dest = dest_row[...]
    owner = lax.div(dest, cells)
    target, slot = owner - my_rank(), dest - owner * cells
    stay = jnp.where(target == 0, slot, -1)
    stay_ref[...] = stay
    leaving = [target == -1, target == 1]
    marks = [as_f32(mask) for mask in leaving]
    stacked = jnp.concatenate(
        [mark[:, t * LANES : (t + 1) * LANES] for mark in marks for t in range(tiles)], 0
    )
    first = lax.broadcasted_iota(jnp.int32, (LANES, LANES), 0)
    second = lax.broadcasted_iota(jnp.int32, (LANES, LANES), 1)
    counts = dot(as_bf16(stacked), as_bf16(jnp.where(first <= second, 1.0, 0.0)))
    places = []
    for side in range(2):
        base = jnp.zeros((1, 1), jnp.float32)
        line = []
        for t in range(tiles):
            row = counts[side * tiles + t : side * tiles + t + 1]
            line.append(row + base)
            base = base + row[:, LANES - 1 :]
        places.append(jnp.concatenate(line, 1).astype(jnp.int32) - 1)
    place = jnp.where(leaving[0], places[0], jnp.where(leaving[1], MOVE + places[1], -1))
    chosen = one_hot(place, 2 * MOVE)
    lists = as_f32(send[...])
    columns = jnp.concatenate([lists, jnp.zeros((6, lists.shape[1]), jnp.float32)], 0).T
    stay_row = as_f32(stay)
    kept = [as_bf16(jnp.where(columns[:, side : side + 1] == stay_row, 1.0, 0.0)) for side in range(2)]
    for copy in copies[2:]:
        copy.wait()
    payload_ref[:BLOCK] = rhs[...]
    payload_ref[BLOCK : BLOCK + 1] = cond[...]
    payload_ref[BLOCK + 1 : BLOCK + 2] = as_f32(slot + 1)
    payload_ref[BLOCK + 2 : ROWS] = jnp.zeros((ROWS - BLOCK - 2, cells), jnp.float32)
    payload = payload_ref[...]
    out = dot_rows(chosen, jnp.concatenate(parts_of(payload, 2), 0))
    packed = out[:, :ROWS] + out[:, ROWS:]
    packed_ref[...] = packed
    traces = face_rows(times3(trace[...], payload), cond[...], 2)
    sides = []
    for side in range(2):
        out = dot_rows(jnp.concatenate(parts_of(traces[side], 2), 0), kept[side])
        ghosts = out[:SLAB] + out[SLAB:]
        row = lax.broadcasted_iota(jnp.int32, (SLAB, 1), 0)
        ghosts = jnp.where(row == FACE + 1, lists[side : side + 1] + 1.0, ghosts)
        moving = packed[side * MOVE : (side + 1) * MOVE]
        half = MOVE // 2
        sides.append(jnp.concatenate([ghosts, jnp.concatenate([moving[:half], moving[half:]], 1)], 0))
    near_up_ref[...] = sides[1]
    near_down_ref[...] = sides[0]
    far_up_ref[...] = packed[MOVE:]
    far_down_ref[...] = packed[:MOVE]


def stay_kernel(count, *refs):
    far, (payload_ref, stay_ref, send_ref, neighbour_ref) = refs[:count], refs[count : count + 4]
    placed_ref, send_hot_ref, ghost_hot_ref, hot_ref = refs[count + 4 : count + 8]
    close, sems = refs[count + 8 : -1], refs[-1]
    copies = [pltpu.make_async_copy(far[k], close[k], sems.at[k]) for k in range(count)]
    for copy in copies:
        copy.start()
    cells = stay_ref.shape[1]
    ghosts = send_ref.shape[1]
    out = dot_rows(jnp.concatenate(parts_of(payload_ref[...], 3), 0), one_hot(stay_ref[...], cells))
    placed_ref[...] = out[:ROWS] + (out[ROWS : 2 * ROWS] + out[2 * ROWS :])
    for side in range(2):
        send_hot_ref[side] = one_hot(send_ref[side : side + 1], cells)
        ghost_hot_ref[side] = one_hot(neighbour_ref[side : side + 1], ghosts, cells + side * ghosts)
    for face in range(FACES):
        hot_ref[face] = one_hot(neighbour_ref[face : face + 1], cells)
    for copy in copies:
        copy.wait()


def face_rows(out, kappa, count):
    row = lax.broadcasted_iota(jnp.int32, (HALF, 1), 0)
    slabs = []
    for face in range(count):
        start = face * SLAB
        values = jnp.where(row == FACE, kappa, out[start : start + HALF])
        slabs.append(jnp.concatenate([values, kappa * out[start + HALF : start + SLAB]], 0))
    return slabs


def moved_ghosts(records, lists, trace_ref):
    columns = records.T
    slabs = face_rows(times3(trace_ref[...], columns), columns[BLOCK : BLOCK + 1], 2)
    slots = records[:, BLOCK + 1 : BLOCK + 2]
    side_of = lax.broadcasted_iota(jnp.int32, (2 * MOVE, 1), 0) // MOVE
    found = []
    for side in range(2):
        wanted = jnp.where(side_of == side, slots, -1.0)
        found.append(pick(slabs[1 - side], as_bf16(jnp.where(wanted == lists[side], 1.0, 0.0)), 2))
    return found


def face_jumps(face, near, own, kappa, neighbour_ref, code_ref, flips):
    code = code_ref[face : face + 1]
    first = 1.0 - 2.0 * as_f32(jnp.bitwise_and(code, 1))
    second = 1.0 - 2.0 * as_f32(jnp.right_shift(code, 1))
    sign = jnp.where(flips[:HALF, 0:1] > 0.0, first, 1.0) * jnp.where(flips[:HALF, 1:2] > 0.0, second, 1.0)
    outside = jnp.where(neighbour_ref[face : face + 1] < 0, 2.0, 1.0)
    strength = PENALTY * jnp.maximum(kappa, near[FACE : FACE + 1])
    values = outside * own[:HALF] - sign * near[:HALF]
    return values, outside * own[HALF:] - sign * near[HALF:], strength


def face_terms(jumps, kappa):
    values, fluxes, strength = jumps
    return jnp.concatenate([strength * values - 0.5 * fluxes, kappa * values], 0)


def one_sided(jumps, own):
    values, fluxes, strength = jumps
    return own[:HALF] * (strength * values - 0.5 * fluxes) - 0.5 * own[HALF:] * values


def both_sided(jumps):
    values, fluxes, strength = jumps
    return values * (strength * values - fluxes)


def first_kernel(placed_ref, near_up_ref, near_down_ref, far_up_ref, far_down_ref, packed_ref, pair_trace_ref,
                 neighbour_ref, code_ref, trace_ref, back_ref, back_ghost_ref, weight_ref, flip_ref, send_hot_ref,
                 ghost_hot_ref, hot_ref, field_ref, kappa_ref, image_ref, pair_ref, right_ref):
    cells = placed_ref.shape[1]
    buffers = (near_up_ref[...], near_down_ref[...])
    records = jnp.concatenate(
        [piece for buffer in buffers for piece in (buffer[SLAB:, :LANES], buffer[SLAB:, LANES:])], 0
    )
    slot = records[:, BLOCK + 1 : BLOCK + 2].astype(jnp.int32) - 1
    ids = lax.broadcasted_iota(jnp.int32, (2 * MOVE, cells), 1)
    merged = placed_ref[...] + pick(records.T, as_bf16(jnp.where(ids == slot, 1.0, 0.0)), 2)
    kappa = merged[BLOCK : BLOCK + 1]
    row = lax.broadcasted_iota(jnp.int32, (ROWS, 1), 0)
    field = jnp.where(row < BLOCK, merged, 0.0)
    field_ref[...] = field
    kappa_ref[...] = kappa
    pair = face_rows(times3(pair_trace_ref[...], field), kappa, 2)
    out = times3(trace_ref[...], field)
    slabs = pair + face_rows(out, kappa, FACES - 2)
    lists = [buffer[FACE + 1 : FACE + 2] for buffer in buffers]
    far = jnp.concatenate([far_up_ref[...], far_down_ref[...]], 0)
    moved = [moved_ghosts(some, lists, pair_trace_ref) for some in (packed_ref[...], far)]
    flips = flip_ref[...]
    terms = []
    for face in range(FACES):
        near = pick(slabs[face ^ 1], hot_ref[face], 2)
        if face < 2:
            ghosts = buffers[face][:SLAB] + (moved[0][face] + moved[1][face])
            near = near + pick(ghosts, ghost_hot_ref[face], 2)
        jumps = face_jumps(face, near, slabs[face], kappa, neighbour_ref, code_ref, flips)
        terms.append(face_terms(jumps, kappa))
    volume = weight_ref[...] * field + kappa * out[(FACES - 2) * SLAB :]
    image = (volume + times3(back_ref[...], jnp.concatenate(terms[2:], 0))
             + times3(back_ghost_ref[...], jnp.concatenate(terms[:2], 0)))
    image_ref[...] = image
    pair_ref[:SLAB], pair_ref[SLAB:] = face_rows(times3(pair_trace_ref[...], image), kappa, 2)
    right_ref[...] = pick(pair_ref[SLAB:], send_hot_ref[1], 2)


def whole_sum(value):
    return jnp.sum(jnp.sum(value, axis=0, keepdims=True), axis=1, keepdims=True)


def second_kernel(image_ref, kappa_ref, pair_ref, neighbour_ref, code_ref, trace_ref, back_ref, weight_ref,
                  flip_ref, hot_ref, send_hot_ref, field_ref, part_ref, near_ref, sums_ref, left_ref):
    left_ref[...] = pick(pair_ref[:SLAB], send_hot_ref[0], 2)
    cells = image_ref.shape[1]
    kappa = kappa_ref[...]
    flips = flip_ref[...]
    field, image = field_ref[...], image_ref[...]
    out = times3(trace_ref[...], image)
    slabs = face_rows(out, kappa, FACES - 2)
    total = jnp.zeros((HALF, cells), jnp.float32)
    terms = []
    for face in range(FACES):
        slab = pair_ref[(1 - face) * SLAB : (2 - face) * SLAB] if face < 2 else slabs[(face ^ 1) - 2]
        near = pick(slab, hot_ref[face], 2)
        if face < 2:
            near_ref[face * SLAB : (face + 1) * SLAB] = near
        if face == 0:
            continue
        own = pair_ref[SLAB:] if face == 1 else slabs[face - 2]
        jumps = face_jumps(face, near, own, kappa, neighbour_ref, code_ref, flips)
        share = one_sided(jumps, own)
        if face == 1:
            total = total + jnp.where(neighbour_ref[1:2] < cells, share, 0.0)
        else:
            total = total + share
            terms.append(face_terms(jumps, kappa))
    volume = weight_ref[...] * image + kappa * out[(FACES - 2) * SLAB :]
    part_ref[...] = volume + times3(back_ref[...], jnp.concatenate(terms, 0))
    totals = (whole_sum(field * field), whole_sum(field * image), whole_sum(image * image),
              whole_sum(image * volume) + whole_sum(flips[:HALF, 2:3] * total))
    lane = lax.broadcasted_iota(jnp.int32, (1, LANES), 1)
    sums = jnp.zeros((1, LANES), jnp.float32)
    for place, value in enumerate(totals):
        sums = jnp.where(lane == place, value, sums)
    sums_ref[...] = sums


def ghost_jumps(face, ghosts, near_ref, pair_ref, kappa, neighbour_ref, code_ref, flips, ghost_hot_ref):
    rows = slice(face * SLAB, (face + 1) * SLAB)
    near = near_ref[rows] + pick(ghosts, ghost_hot_ref[face], 2)
    return face_jumps(face, near, pair_ref[rows], kappa, neighbour_ref, code_ref, flips)


def energy_kernel(near_ref, pair_ref, kappa_ref, from_left_ref, neighbour_ref, code_ref, flip_ref,
                  ghost_hot_ref, partial_ref, sums_ref, term_ref):
    cells = near_ref.shape[1]
    kappa = kappa_ref[...]
    flips = flip_ref[...]
    jumps = ghost_jumps(0, from_left_ref[...], near_ref, pair_ref, kappa, neighbour_ref, code_ref, flips,
                        ghost_hot_ref)
    term_ref[...] = face_terms(jumps, kappa)
    shared = jnp.where(neighbour_ref[0:1] < cells, one_sided(jumps, pair_ref[:SLAB]), both_sided(jumps))
    total = whole_sum(flips[:HALF, 2:3] * shared)
    lane = lax.broadcasted_iota(jnp.int32, (1, LANES), 1)
    sums = partial_ref[...] + jnp.where(lane == 3, total, 0.0)
    sums_ref[...] = jnp.broadcast_to(sums, sums_ref.shape)


def update_kernel(sums_ref, field_ref, image_ref, part_ref, edge_ref, near_ref, pair_ref, kappa_ref,
                  from_right_ref, neighbour_ref, code_ref, back_ref, flip_ref, ghost_hot_ref,
                  solution_hbm, residual_hbm, solution, residual, sems):
    sums = sums_ref[...]
    bb, bw, ww, wt = (sums[:, place : place + 1] for place in range(4))
    alpha = bb / bw
    rr = bb - 2.0 * alpha * bw + alpha * alpha * ww
    beta = rr / bb
    more = 1.0 + beta
    inner = more * more * bw - 2.0 * alpha * more * ww + alpha * alpha * wt
    step = rr / inner
    field, image = field_ref[:BLOCK], image_ref[:BLOCK]
    solution[...] = (alpha + step * more) * field - (step * alpha) * image
    first = pltpu.make_async_copy(solution, solution_hbm, sems.at[0])
    first.start()
    kappa = kappa_ref[...]
    jumps = ghost_jumps(1, from_right_ref[...], near_ref, pair_ref, kappa, neighbour_ref, code_ref,
                        flip_ref[...], ghost_hot_ref)
    edges = jnp.concatenate([edge_ref[...], face_terms(jumps, kappa)], 0)
    twice = part_ref[...] + times3(back_ref[...], edges)
    residual[...] = field - (alpha + step * more) * image + (step * alpha) * twice[:BLOCK]
    second = pltpu.make_async_copy(residual, residual_hbm, sems.at[1])
    second.start()
    first.wait()
    second.wait()


def shift(value, distance):
    count = lax.axis_size(AXES)
    return lax.ppermute(value, AXES, [(i, (i + distance) % count) for i in range(count)])


def bf16(*shape):
    return jax.ShapeDtypeStruct(shape, jnp.bfloat16)


def i32(*shape):
    return jax.ShapeDtypeStruct(shape, jnp.int32)


def body(right_side, conductivity, destination, neighbour, orientation, send_list):
    constants = (jnp.asarray(table) for table in operator_constants())
    trace_pair, trace_rest, back_ghost, back_local, weight_rows, flips = constants
    devices = lax.axis_size(AXES)
    cells = destination.shape[0]
    ghosts = send_list.shape[1]
    whole, slab, row = f32(ROWS, cells), f32(SLAB, ghosts), f32(1, cells)
    pair = f32(2 * SLAB, cells)
    big = 2 * ROWS * cells
    near_up, near_down, far_up, far_down, packed, payload, stay, send, nbr, trace_pair = call(
        pack_kernel,
        [f32(SLAB + MOVE // 2, ghosts)] * 2 + [f32(MOVE, ROWS)] * 2
        + [f32(2 * MOVE, ROWS), whole, i32(1, cells), i32(2, ghosts), i32(FACES, cells), bf16(*trace_pair.shape)],
        [right_side, conductivity[None], destination[None], send_list, trace_pair, neighbour], big * LANES * 6,
        [pltpu.VMEM((BLOCK, cells), jnp.float32), pltpu.VMEM((1, cells), jnp.float32),
         pltpu.VMEM((1, cells), jnp.int32), pltpu.SemaphoreType.DMA((6,))],
        far=6)
    near_up = shift(near_up, 1)
    far_up = shift(far_up, 2)
    far_down = shift(far_down, -2)
    near_down = shift(near_down, -1)
    later = [orientation, trace_rest, back_local, back_ghost, weight_rows, flips]
    placed, send_hot, ghost_hot, hot, *later = call(
        functools.partial(stay_kernel, len(later)),
        [whole, bf16(2, cells, ghosts), bf16(2, ghosts, cells), bf16(FACES, cells, cells)]
        + [jax.ShapeDtypeStruct(a.shape, a.dtype) for a in later],
        later + [payload, stay, send, nbr], big * cells * 3, [pltpu.SemaphoreType.DMA((len(later),))],
        far=len(later))
    orientation, trace_rest, back_local, back_ghost, weight_rows, flips = later
    field, kappa, image, faces, right = call(
        first_kernel, [whole, row, whole, pair, slab],
        [placed, near_up, near_down, far_up, far_down, packed, trace_pair, nbr, orientation, trace_rest,
         back_local, back_ghost, weight_rows, flips, send_hot, ghost_hot, hot],
        big * cells * FACES * 2, ())
    from_left = shift(right, 1)
    part, near, partial, left = call(
        second_kernel, [whole, pair, f32(1, LANES), slab],
        [image, kappa, faces, nbr, orientation, trace_rest, back_local, weight_rows, flips, hot, send_hot, field],
        big * cells * FACES * 2, ())
    from_right = shift(left, -1)
    sums, edge = call(
        energy_kernel, [f32(devices, LANES), f32(SLAB, cells)],
        [near, faces, kappa, from_left, nbr, orientation, flips, ghost_hot, partial],
        big * SLAB * 2, ())
    sums = lax.all_to_all(sums, AXES, 0, 0, tiled=True)
    total = jnp.sum(sums, axis=0, keepdims=True)
    return tuple(call(
        update_kernel, [f32(BLOCK, cells)] * 2,
        [total, field, image, part, edge, near, faces, kappa, from_right, nbr, orientation, back_ghost, flips,
         ghost_hot], big * 2 * SLAB * 3,
        [pltpu.VMEM((BLOCK, cells), jnp.float32)] * 2 + [pltpu.SemaphoreType.DMA((2,))], out=pltpu.MemorySpace.HBM))


def solution(mesh):
    in_specs = (
        P(None, AXES),
        P(AXES),
        P(AXES),
        P(None, AXES),
        P(None, AXES),
        P(None, AXES),
    )
    out_specs = (P(None, AXES), P(None, AXES))
    return jax.shard_map(body, mesh=mesh, in_specs=in_specs, out_specs=out_specs, check_vma=False)
```

profile of v0, /device:TPU:0, one launch (start us, length us, event | category | flops | bytes accessed | tf_op | source)
XLA Modules:
  0.0 35.3 jit_solution(18300584365675955216)
XLA Ops:
  0.6 1.5 %shard_map.131 = (f32[96,256]{1,0:T(8,128)S(1)}, f32[96,256]{1,0:T(8,128)S(1)}, f32[64,128]{1,0:T(8,128)S(1)}, f32[64,128]{1,0:T(8,128)S(1)}, f32[128,128]{1,0:T...) custom-call(f32[125,512]{1,0:T(8,128)} %rhs_hbm.1, ...), custom_call_target="tpu_custom_call" | custom-call | flops 100663296 | bytes 1077248 | tf_op jit(solution)/shard_map/pallas_call | solution.py:181
  2.2 3.0 %collective-permute-start = (f32[96,256]{1,0:T(8,128)S(1)}, f32[96,256]{1,0:T(8,128)S(1)}, u32[]{:S(2)}, u32[]{:S(2)}) collective-permute-start(f32[96,256]{1,0:T(8,128)S(1)} %get-tuple-element.38), channel_id=1, source_target_pairs={{0,1},{1,2},{2,3},{3,4},{4,5},{5,6},{6,7},{7,8},{8,9},{9,10},{10,1... | collective-permute-start | bytes 294920 | tf_op jit(solution)/shard_map/ppermute | solution.py:467
  5.2 3.5 %collective-permute-start.1 = (f32[96,256]{1,0:T(8,128)S(1)}, f32[96,256]{1,0:T(8,128)S(1)}, u32[]{:S(2)}, u32[]{:S(2)}) collective-permute-start(f32[96,256]{1,0:T(8,128)S(1)} %get-tuple-element.39), channel_id=1, source_target_pairs={{0,31},{1,0},{2,1},{3,2},{4,3},{5,4},{6,5},{7,6},{8,7},{9,8},{10,9... | collective-permute-start | bytes 294920 | tf_op jit(solution)/shard_map/ppermute | solution.py:467
  8.7 0.0 collective-permute-start.2
  8.7 4.4 %collective-permute-start.3 = (f32[64,128]{1,0:T(8,128)S(1)}, f32[64,128]{1,0:T(8,128)S(1)}, u32[]{:S(2)}, u32[]{:S(2)}) collective-permute-start(f32[64,128]{1,0:T(8,128)S(1)} %get-tuple-element.41), channel_id=1, source_target_pairs={{0,30},{1,31},{2,0},{3,1},{4,2},{5,3},{6,4},{7,5},{8,6},{9,7},{10,... | collective-permute-start | bytes 98312 | tf_op jit(solution)/shard_map/ppermute | solution.py:467
  13.2 1.1 %shard_map.132 = (f32[128,512]{1,0:T(8,128)S(1)}, bf16[2,512,256]{2,1,0:T(8,128)(2,1)S(1)}, bf16[2,256,512]{2,1,0:T(8,128)(2,1)S(1)}, bf16[6,512,512]{2,1,0:T(8,...) custom-call(s32[6,512]{1,0:T(8,128)} %refs_0_.1, ...), custom_call_target="tpu_custom_call" | custom-call | flops 201326592 | bytes 6005760 | tf_op jit(solution)/shard_map/pallas_call | solution.py:181
  14.3 0.8 %collective-permute-done.2.far_up_ref = f32[64,128]{1,0:T(8,128)S(1)} collective-permute-done((f32[64,128]{1,0:T(8,128)S(1)}, f32[64,128]{1,0:T(8,128)S(1)}, u32[]{:S(2)}, u32[]{:S(2)}) %collective-permute-start.2) | collective-permute-done | bytes 32800 | tf_op jit(solution)/shard_map/ppermute | solution.py:467
  15.1 0.0 collective-permute-done.3.far_down_ref
  15.1 0.0 collective-permute-done.near_up_ref
  15.1 0.0 collective-permute-done.1.near_down_ref
  15.1 2.4 %shard_map.133 = (f32[128,512]{1,0:T(8,128)S(1)}, f32[1,512]{1,0:T(1,128)S(1)}, f32[128,512]{1,0:T(8,128)S(1)}, f32[128,512]{1,0:T(8,128)S(1)}, f32[64,256]{1,0:T(8,128)S(1)}) custom-call(f32[128,512]{1,0:T(8,128)S(1)} %get-tuple-element.37.placed_ref, f32[96,256]{1,0:T(8,128)S(1)} %collective-permute-done.near_up_ref, ...), custom_call_target="tpu_custom_call" | custom-call | flops 805306368 | bytes 6384128 | tf_op jit(solution)/shard_map/pallas_call | solution.py:181
  17.5 0.1 collective-permute-start.4
  17.6 1.3 %shard_map.134 = (f32[128,512]{1,0:T(8,128)S(1)}, f32[128,512]{1,0:T(8,128)S(1)}, f32[1,128]{1,0:T(1,128)S(1)}, f32[64,256]{1,0:T(8,128)S(1)}) custom-call(f32[128,512]{1,0:T(8,128)S(1)} %get-tuple-element.53.image_ref, f32[1,512]{1,0:T(1,128)S(1)} %get-tuple-element.54.kappa_ref, f32[128,512]{1,0:T(8,128)S(1)} %get-tuple-element.55.pair_ref, ...), custom_call_target="tpu_custom_call" | custom-call | flops 805306368 | bytes 5598208 | tf_op jit(solution)/shard_map/pallas_call | solution.py:181
  19.0 5.4 %collective-permute-start.5 = (f32[64,256]{1,0:T(8,128)S(1)}, f32[64,256]{1,0:T(8,128)S(1)}, u32[]{:S(2)}, u32[]{:S(2)}) collective-permute-start(f32[64,256]{1,0:T(8,128)S(1)} %get-tuple-element.63), channel_id=1, source_target_pairs={{0,31},{1,0},{2,1},{3,2},{4,3},{5,4},{6,5},{7,6},{8,7},{9,8},{10,9... | collective-permute-start | bytes 196616 | tf_op jit(solution)/shard_map/ppermute | solution.py:467
  24.3 0.6 %collective-permute-done.4.from_left_ref = f32[64,256]{1,0:T(8,128)S(1)} collective-permute-done((f32[64,256]{1,0:T(8,128)S(1)}, f32[64,256]{1,0:T(8,128)S(1)}, u32[]{:S(2)}, u32[]{:S(2)}) %collective-permute-start.4) | collective-permute-done | bytes 65568 | tf_op jit(solution)/shard_map/ppermute | solution.py:467
  24.9 0.3 shard_map.135
  25.2 8.8 %all_to_all.9 = f32[32,1,128]{2,1,0:T(1,128)S(1)} all-to-all(f32[32,1,128]{2,1,0:T(1,128)S(1)} %bitcast.6), channel_id=1, replica_groups=mesh['curve'=4,'group'=8] {'curve','group'}, dimensions={0} | all-to-all | bytes 32768 | tf_op jit(solution)/shard_map/all_to_all | solution.py:522
  34.0 0.1 reduce_sum.9
  34.1 0.0 collective-permute-done.5.from_right_ref
  34.1 1.2 %shard_map.136 = (f32[125,512]{1,0:T(8,128)}, f32[125,512]{1,0:T(8,128)}) custom-call(f32[1,128]{1,0:T(1,128)S(1)} %bitcast.7, f32[128,512]{1,0:T(8,128)S(1)} %get-tuple-element.56.field_ref, f32[128,512]{1,0:T(8,128)S(1)} %get-tuple-element.53.image_ref, f32[128,512]{1,0:T(8,128)S(1)} %get-tuple-element.61.part_ref, ...), custom_call_target="tpu_custom_call" | custom-call | flops 50331648 | bytes 2701824 | tf_op jit(solution)/shard_map/pallas_call | solution.py:181
Async XLA Ops:
  2.2 12.9 %collective-permute-start = (f32[96,256]{1,0:T(8,128)S(1)}, f32[96,256]{1,0:T(8,128)S(1)}, u32[]{:S(2)}, u32[]{:S(2)}) collective-permute-start(f32[96,256]{1,0:T(8,128)S(1)} %get-tuple-element.38), channel_id=1, source_target_pairs={{0,1},{1,2},{2,3},{3,4},{4,5},{5,6},{6,7},{7,8},{8,9},{9,10},{10,1... | collective-permute-start | bytes 294920 | tf_op jit(solution)/shard_map/ppermute | solution.py:467
  5.2 9.9 %collective-permute-start.1 = (f32[96,256]{1,0:T(8,128)S(1)}, f32[96,256]{1,0:T(8,128)S(1)}, u32[]{:S(2)}, u32[]{:S(2)}) collective-permute-start(f32[96,256]{1,0:T(8,128)S(1)} %get-tuple-element.39), channel_id=1, source_target_pairs={{0,31},{1,0},{2,1},{3,2},{4,3},{5,4},{6,5},{7,6},{8,7},{9,8},{10,9... | collective-permute-start | bytes 294920 | tf_op jit(solution)/shard_map/ppermute | solution.py:467
  8.7 6.4 %collective-permute-start.2 = (f32[64,128]{1,0:T(8,128)S(1)}, f32[64,128]{1,0:T(8,128)S(1)}, u32[]{:S(2)}, u32[]{:S(2)}) collective-permute-start(f32[64,128]{1,0:T(8,128)S(1)} %get-tuple-element.40), channel_id=1, source_target_pairs={{0,2},{1,3},{2,4},{3,5},{4,6},{5,7},{6,8},{7,9},{8,10},{9,11},{10,... | collective-permute-start | bytes 98312 | tf_op jit(solution)/shard_map/ppermute | solution.py:467
  8.7 6.4 %collective-permute-start.3 = (f32[64,128]{1,0:T(8,128)S(1)}, f32[64,128]{1,0:T(8,128)S(1)}, u32[]{:S(2)}, u32[]{:S(2)}) collective-permute-start(f32[64,128]{1,0:T(8,128)S(1)} %get-tuple-element.41), channel_id=1, source_target_pairs={{0,30},{1,31},{2,0},{3,1},{4,2},{5,3},{6,4},{7,5},{8,6},{9,7},{10,... | collective-permute-start | bytes 98312 | tf_op jit(solution)/shard_map/ppermute | solution.py:467
  17.5 7.3 %collective-permute-start.4 = (f32[64,256]{1,0:T(8,128)S(1)}, f32[64,256]{1,0:T(8,128)S(1)}, u32[]{:S(2)}, u32[]{:S(2)}) collective-permute-start(f32[64,256]{1,0:T(8,128)S(1)} %get-tuple-element.58), channel_id=1, source_target_pairs={{0,1},{1,2},{2,3},{3,4},{4,5},{5,6},{6,7},{7,8},{8,9},{9,10},{10,1... | collective-permute-start | bytes 196616 | tf_op jit(solution)/shard_map/ppermute | solution.py:467
  19.0 15.1 %collective-permute-start.5 = (f32[64,256]{1,0:T(8,128)S(1)}, f32[64,256]{1,0:T(8,128)S(1)}, u32[]{:S(2)}, u32[]{:S(2)}) collective-permute-start(f32[64,256]{1,0:T(8,128)S(1)} %get-tuple-element.63), channel_id=1, source_target_pairs={{0,31},{1,0},{2,1},{3,2},{4,3},{5,4},{6,5},{7,6},{8,7},{9,8},{10,9... | collective-permute-start | bytes 196616 | tf_op jit(solution)/shard_map/ppermute | solution.py:467
where the time goes:
time: 35.5 us; the launch traced here: 35.3 us
  starting transfers between devices  16.4 us (46%)
  blocking collectives  8.84 us (25%)
  Pallas kernels  7.94 us (22%)
  waiting for transfers between devices  1.35 us (4%)
  between operations  0.68 us (2%)
    ppermute x6, starting transfers between devices, shift(): lax.ppermute(value, AXES, [(i, (i + distance) % count) for i in range(cou...  16.4 us
    all_to_all x1, blocking collectives, body(): sums = lax.all_to_all(sums, AXES, 0, 0, tiled=True)  8.84 us
    pallas_call x6, Pallas kernels, call(): pl.pallas_call(kernel, out_shape=list(outs), in_specs=[pl.BlockSpec(memor...  7.94 us
    ppermute x6, waiting for transfers between devices, shift(): lax.ppermute(value, AXES, [(i, (i + distance) % count) for i in range(cou...  1.35 us
  transfers between devices with their start and end apart: 6, of which 2 were waited for; matrix products, arithmetic and copies ran while one was open for 0% of the time, Pallas kernels for 8%

commit v1 on v0

--- a/solution.py
+++ b/solution.py
@@ -17,6 +17,7 @@
 ROWS = 128
 HALF = 32
 SLAB = 2 * HALF
+THIN = 56
 FACES = 6
 PENALTY = 80.0
 AXES = ("curve", "group")
@@ -267,16 +268,17 @@
 
 
 def stay_kernel(count, *refs):
-    far, (payload_ref, stay_ref, send_ref, neighbour_ref) = refs[:count], refs[count : count + 4]
-    placed_ref, send_hot_ref, ghost_hot_ref, hot_ref = refs[count + 4 : count + 8]
-    close, sems = refs[count + 8 : -1], refs[-1]
+    far, (payload_ref, stay_ref, send_ref, neighbour_ref, pair_trace_ref) = refs[:count], refs[count : count + 5]
+    placed_ref, send_hot_ref, ghost_hot_ref, hot_ref, slab_ref, beside_ref, stiff_ref = refs[count + 5 : count + 12]
+    close, sems = refs[count + 12 : -1], refs[-1]
     copies = [pltpu.make_async_copy(far[k], close[k], sems.at[k]) for k in range(count)]
     for copy in copies:
         copy.start()
     cells = stay_ref.shape[1]
     ghosts = send_ref.shape[1]
     out = dot_rows(jnp.concatenate(parts_of(payload_ref[...], 3), 0), one_hot(stay_ref[...], cells))
-    placed_ref[...] = out[:ROWS] + (out[ROWS : 2 * ROWS] + out[2 * ROWS :])
+    placed = out[:ROWS] + (out[ROWS : 2 * ROWS] + out[2 * ROWS :])
+    placed_ref[...] = placed
     for side in range(2):
         send_hot_ref[side] = one_hot(send_ref[side : side + 1], cells)
         ghost_hot_ref[side] = one_hot(neighbour_ref[side : side + 1], ghosts, cells + side * ghosts)
@@ -284,6 +286,11 @@
         hot_ref[face] = one_hot(neighbour_ref[face : face + 1], cells)
     for copy in copies:
         copy.wait()
+    slabs, stiff = all_faces(placed, placed[BLOCK : BLOCK + 1], pair_trace_ref, close[1])
+    stiff_ref[...] = stiff
+    for face in range(FACES):
+        slab_ref[face * SLAB : (face + 1) * SLAB] = slabs[face]
+        beside_ref[face * SLAB : (face + 1) * SLAB] = pick(slabs[face ^ 1], hot_ref[face], 2)
 
 
 def face_rows(out, kappa, count):
@@ -294,6 +301,14 @@
         values = jnp.where(row == FACE, kappa, out[start : start + HALF])
         slabs.append(jnp.concatenate([values, kappa * out[start + HALF : start + SLAB]], 0))
     return slabs
+
+
+def all_faces(field, kappa, pair_trace_ref, trace_ref):
+    high, low = parts_of(field, 2)
+    triple = jnp.concatenate([high, low, high], 0)
+    out = dot(trace_ref[...], triple)
+    slabs = face_rows(dot(pair_trace_ref[...], triple), kappa, 2) + face_rows(out, kappa, FACES - 2)
+    return slabs, kappa * out[(FACES - 2) * SLAB :]
 
 
 def moved_ghosts(records, lists, trace_ref):
@@ -334,43 +349,49 @@
     return values * (strength * values - fluxes)
 
 
-def first_kernel(placed_ref, near_up_ref, near_down_ref, far_up_ref, far_down_ref, packed_ref, pair_trace_ref,
+def first_kernel(placed_ref, slab_ref, beside_ref, stiff_ref, near_up_ref, near_down_ref, far_up_ref, far_down_ref, packed_ref, pair_trace_ref,
                  neighbour_ref, code_ref, trace_ref, back_ref, back_ghost_ref, weight_ref, flip_ref, send_hot_ref,
-                 ghost_hot_ref, hot_ref, field_ref, kappa_ref, image_ref, pair_ref, right_ref):
+                 ghost_hot_ref, field_ref, kappa_ref, image_ref, pair_ref, right_ref):
     cells = placed_ref.shape[1]
     buffers = (near_up_ref[...], near_down_ref[...])
     records = jnp.concatenate(
         [piece for buffer in buffers for piece in (buffer[SLAB:, :LANES], buffer[SLAB:, LANES:])], 0
     )
     slot = records[:, BLOCK + 1 : BLOCK + 2].astype(jnp.int32) - 1
+    slot = jnp.where(slot < 0, -2, slot)
     ids = lax.broadcasted_iota(jnp.int32, (2 * MOVE, cells), 1)
-    merged = placed_ref[...] + pick(records.T, as_bf16(jnp.where(ids == slot, 1.0, 0.0)), 2)
+    arrived = records.T
+    new_slabs, new_stiff = all_faces(arrived, arrived[BLOCK : BLOCK + 1], pair_trace_ref, trace_ref)
+    added = pick(jnp.concatenate([*new_slabs, new_stiff, arrived], 0), as_bf16(jnp.where(ids == slot, 1.0, 0.0)), 2)
+    merged = placed_ref[...] + added[FACES * SLAB + ROWS :]
     kappa = merged[BLOCK : BLOCK + 1]
     row = lax.broadcasted_iota(jnp.int32, (ROWS, 1), 0)
     field = jnp.where(row < BLOCK, merged, 0.0)
     field_ref[...] = field
     kappa_ref[...] = kappa
-    pair = face_rows(times3(pair_trace_ref[...], field), kappa, 2)
-    out = times3(trace_ref[...], field)
-    slabs = pair + face_rows(out, kappa, FACES - 2)
+    slabs = [
+        slab_ref[face * SLAB : (face + 1) * SLAB] + added[face * SLAB : (face + 1) * SLAB] for face in range(FACES)
+    ]
+    stiff = stiff_ref[...] + added[FACES * SLAB : FACES * SLAB + ROWS]
     lists = [buffer[FACE + 1 : FACE + 2] for buffer in buffers]
     far = jnp.concatenate([far_up_ref[...], far_down_ref[...]], 0)
     moved = [moved_ghosts(some, lists, pair_trace_ref) for some in (packed_ref[...], far)]
     flips = flip_ref[...]
     terms = []
     for face in range(FACES):
-        near = pick(slabs[face ^ 1], hot_ref[face], 2)
+        chosen = as_bf16(jnp.where(slot == neighbour_ref[face : face + 1], 1.0, 0.0))
+        near = beside_ref[face * SLAB : (face + 1) * SLAB] + pick(new_slabs[face ^ 1], chosen, 2)
         if face < 2:
             ghosts = buffers[face][:SLAB] + (moved[0][face] + moved[1][face])
             near = near + pick(ghosts, ghost_hot_ref[face], 2)
         jumps = face_jumps(face, near, slabs[face], kappa, neighbour_ref, code_ref, flips)
         terms.append(face_terms(jumps, kappa))
-    volume = weight_ref[...] * field + kappa * out[(FACES - 2) * SLAB :]
+    volume = weight_ref[...] * field + stiff
     image = (volume + times3(back_ref[...], jnp.concatenate(terms[2:], 0))
              + times3(back_ghost_ref[...], jnp.concatenate(terms[:2], 0)))
     image_ref[...] = image
     pair_ref[:SLAB], pair_ref[SLAB:] = face_rows(times3(pair_trace_ref[...], image), kappa, 2)
-    right_ref[...] = pick(pair_ref[SLAB:], send_hot_ref[1], 2)
+    right_ref[...] = squeeze(pick(pair_ref[SLAB:], send_hot_ref[1], 2))
 
 
 def whole_sum(value):
@@ -379,7 +400,7 @@
 
 def second_kernel(image_ref, kappa_ref, pair_ref, neighbour_ref, code_ref, trace_ref, back_ref, weight_ref,
                   flip_ref, hot_ref, send_hot_ref, field_ref, part_ref, near_ref, sums_ref, left_ref):
-    left_ref[...] = pick(pair_ref[:SLAB], send_hot_ref[0], 2)
+    left_ref[...] = squeeze(pick(pair_ref[:SLAB], send_hot_ref[0], 2))
     cells = image_ref.shape[1]
     kappa = kappa_ref[...]
     flips = flip_ref[...]
@@ -414,6 +435,17 @@
     sums_ref[...] = sums
 
 
+def squeeze(slab):
+    idle = jnp.zeros((THIN - 2 * FACE - 1, slab.shape[1]), jnp.float32)
+    return jnp.concatenate([slab[: FACE + 1], slab[HALF : HALF + FACE], idle], 0)
+
+
+def spread(thin):
+    gap = jnp.zeros((HALF - FACE - 1, thin.shape[1]), jnp.float32)
+    tail = jnp.zeros((HALF - FACE, thin.shape[1]), jnp.float32)
+    return jnp.concatenate([thin[: FACE + 1], gap, thin[FACE + 1 : 2 * FACE + 1], tail], 0)
+
+
 def ghost_jumps(face, ghosts, near_ref, pair_ref, kappa, neighbour_ref, code_ref, flips, ghost_hot_ref):
     rows = slice(face * SLAB, (face + 1) * SLAB)
     near = near_ref[rows] + pick(ghosts, ghost_hot_ref[face], 2)
@@ -425,7 +457,7 @@
     cells = near_ref.shape[1]
     kappa = kappa_ref[...]
     flips = flip_ref[...]
-    jumps = ghost_jumps(0, from_left_ref[...], near_ref, pair_ref, kappa, neighbour_ref, code_ref, flips,
+    jumps = ghost_jumps(0, spread(from_left_ref[...]), near_ref, pair_ref, kappa, neighbour_ref, code_ref, flips,
                         ghost_hot_ref)
     term_ref[...] = face_terms(jumps, kappa)
     shared = jnp.where(neighbour_ref[0:1] < cells, one_sided(jumps, pair_ref[:SLAB]), both_sided(jumps))
@@ -451,7 +483,7 @@
     first = pltpu.make_async_copy(solution, solution_hbm, sems.at[0])
     first.start()
     kappa = kappa_ref[...]
-    jumps = ghost_jumps(1, from_right_ref[...], near_ref, pair_ref, kappa, neighbour_ref, code_ref,
+    jumps = ghost_jumps(1, spread(from_right_ref[...]), near_ref, pair_ref, kappa, neighbour_ref, code_ref,
                         flip_ref[...], ghost_hot_ref)
     edges = jnp.concatenate([edge_ref[...], face_terms(jumps, kappa)], 0)
     twice = part_ref[...] + times3(back_ref[...], edges)
@@ -481,7 +513,7 @@
     devices = lax.axis_size(AXES)
     cells = destination.shape[0]
     ghosts = send_list.shape[1]
-    whole, slab, row = f32(ROWS, cells), f32(SLAB, ghosts), f32(1, cells)
+    whole, slab, row = f32(ROWS, cells), f32(THIN, ghosts), f32(1, cells)
     pair = f32(2 * SLAB, cells)
     big = 2 * ROWS * cells
     near_up, near_down, far_up, far_down, packed, payload, stay, send, nbr, trace_pair = call(
@@ -497,17 +529,18 @@
     far_down = shift(far_down, -2)
     near_down = shift(near_down, -1)
     later = [orientation, trace_rest, back_local, back_ghost, weight_rows, flips]
-    placed, send_hot, ghost_hot, hot, *later = call(
+    slabs = f32(FACES * SLAB, cells)
+    placed, send_hot, ghost_hot, hot, slab_rows, beside, stiff, *later = call(
         functools.partial(stay_kernel, len(later)),
-        [whole, bf16(2, cells, ghosts), bf16(2, ghosts, cells), bf16(FACES, cells, cells)]
+        [whole, bf16(2, cells, ghosts), bf16(2, ghosts, cells), bf16(FACES, cells, cells), slabs, slabs, whole]
         + [jax.ShapeDtypeStruct(a.shape, a.dtype) for a in later],
-        later + [payload, stay, send, nbr], big * cells * 3, [pltpu.SemaphoreType.DMA((len(later),))],
+        later + [payload, stay, send, nbr, trace_pair], big * cells * 3, [pltpu.SemaphoreType.DMA((len(later),))],
         far=len(later))
     orientation, trace_rest, back_local, back_ghost, weight_rows, flips = later
     field, kappa, image, faces, right = call(
         first_kernel, [whole, row, whole, pair, slab],
-        [placed, near_up, near_down, far_up, far_down, packed, trace_pair, nbr, orientation, trace_rest,
-         back_local, back_ghost, weight_rows, flips, send_hot, ghost_hot, hot],
+        [placed, slab_rows, beside, stiff, near_up, near_down, far_up, far_down, packed, trace_pair, nbr, orientation, trace_rest,
+         back_local, back_ghost, weight_rows, flips, send_hot, ghost_hot],
         big * cells * FACES * 2, ())
     from_left = shift(right, 1)
     part, near, partial, left = call(

time: 35.5 us -> 36.6 us (1.031)
  Pallas kernels: 7.94 us -> 9.45 us
  waiting for transfers between devices: 1.35 us -> 0.62 us
    pallas_call x6, Pallas kernels: 7.94 us -> 9.45 us  [call(): pl.pallas_call(kernel, out_shape=list(outs), in_specs=[pl.BlockSpec(memor...]
    ppermute x6, waiting for transfers between devices: 1.35 us -> 0.62 us  [shift(): lax.ppermute(value, AXES, [(i, (i + distance) % count) for i in range(cou...]
  transfers between devices with their start and end apart: 6 -> 6, of which waited for: 2 -> 1; matrix products, arithmetic and copies ran while one was open for 0% -> 0% of each run, Pallas kernels for 8% -> 12%
where the time goes in v1:
time: 36.6 us; the launch traced here: 36.4 us
  starting transfers between devices  16.4 us (45%)
  Pallas kernels  9.45 us (26%)
  blocking collectives  9.17 us (25%)
  between operations  0.71 us (2%)
  waiting for transfers between devices  0.62 us (2%)
    ppermute x6, starting transfers between devices, shift(): lax.ppermute(value, AXES, [(i, (i + distance) % count) for i in range(cou...  16.4 us
    pallas_call x6, Pallas kernels, call(): pl.pallas_call(kernel, out_shape=list(outs), in_specs=[pl.BlockSpec(memor...  9.45 us
    all_to_all x1, blocking collectives, body(): sums = lax.all_to_all(sums, AXES, 0, 0, tiled=True)  9.17 us
  transfers between devices with their start and end apart: 6, of which 1 were waited for; matrix products, arithmetic and copies ran while one was open for 0% of the time, Pallas kernels for 12%

profile of v1, /device:TPU:0, one launch (start us, length us, event | category | flops | bytes accessed | tf_op | source)
XLA Modules:
  0.0 36.4 jit_solution(3383571859923198206)
XLA Ops:
  0.6 1.5 %shard_map.131 = (f32[96,256]{1,0:T(8,128)S(1)}, f32[96,256]{1,0:T(8,128)S(1)}, f32[64,128]{1,0:T(8,128)S(1)}, f32[64,128]{1,0:T(8,128)S(1)}, f32[128,128]{1,0:T...) custom-call(f32[125,512]{1,0:T(8,128)} %rhs_hbm.1, ...), custom_call_target="tpu_custom_call" | custom-call | flops 100663296 | bytes 1077248 | tf_op jit(solution)/shard_map/pallas_call | solution.py:182
  2.2 3.0 %collective-permute-start = (f32[96,256]{1,0:T(8,128)S(1)}, f32[96,256]{1,0:T(8,128)S(1)}, u32[]{:S(2)}, u32[]{:S(2)}) collective-permute-start(f32[96,256]{1,0:T(8,128)S(1)} %get-tuple-element.45), channel_id=1, source_target_pairs={{0,1},{1,2},{2,3},{3,4},{4,5},{5,6},{6,7},{7,8},{8,9},{9,10},{10,1... | collective-permute-start | bytes 294920 | tf_op jit(solution)/shard_map/ppermute | solution.py:499
  5.2 3.5 %collective-permute-start.1 = (f32[96,256]{1,0:T(8,128)S(1)}, f32[96,256]{1,0:T(8,128)S(1)}, u32[]{:S(2)}, u32[]{:S(2)}) collective-permute-start(f32[96,256]{1,0:T(8,128)S(1)} %get-tuple-element.46), channel_id=1, source_target_pairs={{0,31},{1,0},{2,1},{3,2},{4,3},{5,4},{6,5},{7,6},{8,7},{9,8},{10,9... | collective-permute-start | bytes 294920 | tf_op jit(solution)/shard_map/ppermute | solution.py:499
  8.7 0.0 collective-permute-start.2
  8.7 4.4 %collective-permute-start.3 = (f32[64,128]{1,0:T(8,128)S(1)}, f32[64,128]{1,0:T(8,128)S(1)}, u32[]{:S(2)}, u32[]{:S(2)}) collective-permute-start(f32[64,128]{1,0:T(8,128)S(1)} %get-tuple-element.48), channel_id=1, source_target_pairs={{0,30},{1,31},{2,0},{3,1},{4,2},{5,3},{6,4},{7,5},{8,6},{9,7},{10,... | collective-permute-start | bytes 98312 | tf_op jit(solution)/shard_map/ppermute | solution.py:499
  13.2 2.8 %shard_map.132 = (f32[128,512]{1,0:T(8,128)S(1)}, bf16[2,512,256]{2,1,0:T(8,128)(2,1)S(1)}, bf16[2,256,512]{2,1,0:T(8,128)(2,1)S(1)}, bf16[6,512,512]{2,1,0:T(8,...) custom-call(s32[6,512]{1,0:T(8,128)} %refs_0_.1, ...), custom_call_target="tpu_custom_call" | custom-call | flops 201326592 | bytes 7939072 | tf_op jit(solution)/shard_map/pallas_call | solution.py:182
  16.0 0.0 collective-permute-done.2.far_up_ref
  16.0 0.0 collective-permute-done.3.far_down_ref
  16.0 0.0 collective-permute-done.near_up_ref
  16.0 0.0 collective-permute-done.1.near_down_ref
  16.0 2.4 %shard_map.133 = (f32[128,512]{1,0:T(8,128)S(1)}, f32[1,512]{1,0:T(1,128)S(1)}, f32[128,512]{1,0:T(8,128)S(1)}, f32[128,512]{1,0:T(8,128)S(1)}, f32[56,256]{1,0:T(8,128)S(1)}) custom-call(f32[128,512]{1,0:T(8,128)S(1)} %get-tuple-element.41.placed_ref, f32[384,512]{1,0:T(8,128)S(1)} %get-tuple-element.42.slab_ref, ...), custom_call_target="tpu_custom_call" | custom-call | flops 805306368 | bytes 5065216 | tf_op jit(solution)/shard_map/pallas_call | solution.py:182
  18.4 0.1 collective-permute-start.4
  18.5 1.2 %shard_map.134 = (f32[128,512]{1,0:T(8,128)S(1)}, f32[128,512]{1,0:T(8,128)S(1)}, f32[1,128]{1,0:T(1,128)S(1)}, f32[56,256]{1,0:T(8,128)S(1)}) custom-call(f32[128,512]{1,0:T(8,128)S(1)} %get-tuple-element.58.image_ref, f32[1,512]{1,0:T(1,128)S(1)} %get-tuple-element.59.kappa_ref, f32[128,512]{1,0:T(8,128)S(1)} %get-tuple-element.60.pair_ref, ...), custom_call_target="tpu_custom_call" | custom-call | flops 805306368 | bytes 5590016 | tf_op jit(solution)/shard_map/pallas_call | solution.py:182
  19.7 5.4 %collective-permute-start.5 = (f32[56,256]{1,0:T(8,128)S(1)}, f32[56,256]{1,0:T(8,128)S(1)}, u32[]{:S(2)}, u32[]{:S(2)}) collective-permute-start(f32[56,256]{1,0:T(8,128)S(1)} %get-tuple-element.69), channel_id=1, source_target_pairs={{0,31},{1,0},{2,1},{3,2},{4,3},{5,4},{6,5},{7,6},{8,7},{9,8},{10,9... | collective-permute-start | bytes 172040 | tf_op jit(solution)/shard_map/ppermute | solution.py:499
  25.1 0.6 %collective-permute-done.4.from_left_ref = f32[56,256]{1,0:T(8,128)S(1)} collective-permute-done((f32[56,256]{1,0:T(8,128)S(1)}, f32[56,256]{1,0:T(8,128)S(1)}, u32[]{:S(2)}, u32[]{:S(2)}) %collective-permute-start.4) | collective-permute-done | bytes 57376 | tf_op jit(solution)/shard_map/ppermute | solution.py:499
  25.7 0.3 shard_map.135
  26.0 9.2 %all_to_all.9 = f32[32,1,128]{2,1,0:T(1,128)S(1)} all-to-all(f32[32,1,128]{2,1,0:T(1,128)S(1)} %bitcast.6), channel_id=1, replica_groups=mesh['curve'=4,'group'=8] {'curve','group'}, dimensions={0} | all-to-all | bytes 32768 | tf_op jit(solution)/shard_map/all_to_all | solution.py:555
  35.2 0.1 reduce_sum.9
  35.2 0.0 collective-permute-done.5.from_right_ref
  35.2 1.2 %shard_map.136 = (f32[125,512]{1,0:T(8,128)}, f32[125,512]{1,0:T(8,128)}) custom-call(f32[1,128]{1,0:T(1,128)S(1)} %bitcast.7, f32[128,512]{1,0:T(8,128)S(1)} %get-tuple-element.62.field_ref, f32[128,512]{1,0:T(8,128)S(1)} %get-tuple-element.58.image_ref, f32[128,512]{1,0:T(8,128)S(1)} %get-tuple-element.67.part_ref, ...), custom_call_target="tpu_custom_call" | custom-call | flops 50331648 | bytes 2693632 | tf_op jit(solution)/shard_map/pallas_call | solution.py:182
Async XLA Ops:
  2.2 13.8 %collective-permute-start = (f32[96,256]{1,0:T(8,128)S(1)}, f32[96,256]{1,0:T(8,128)S(1)}, u32[]{:S(2)}, u32[]{:S(2)}) collective-permute-start(f32[96,256]{1,0:T(8,128)S(1)} %get-tuple-element.45), channel_id=1, source_target_pairs={{0,1},{1,2},{2,3},{3,4},{4,5},{5,6},{6,7},{7,8},{8,9},{9,10},{10,1... | collective-permute-start | bytes 294920 | tf_op jit(solution)/shard_map/ppermute | solution.py:499
  5.2 10.8 %collective-permute-start.1 = (f32[96,256]{1,0:T(8,128)S(1)}, f32[96,256]{1,0:T(8,128)S(1)}, u32[]{:S(2)}, u32[]{:S(2)}) collective-permute-start(f32[96,256]{1,0:T(8,128)S(1)} %get-tuple-element.46), channel_id=1, source_target_pairs={{0,31},{1,0},{2,1},{3,2},{4,3},{5,4},{6,5},{7,6},{8,7},{9,8},{10,9... | collective-permute-start | bytes 294920 | tf_op jit(solution)/shard_map/ppermute | solution.py:499
  8.7 7.3 %collective-permute-start.2 = (f32[64,128]{1,0:T(8,128)S(1)}, f32[64,128]{1,0:T(8,128)S(1)}, u32[]{:S(2)}, u32[]{:S(2)}) collective-permute-start(f32[64,128]{1,0:T(8,128)S(1)} %get-tuple-element.47), channel_id=1, source_target_pairs={{0,2},{1,3},{2,4},{3,5},{4,6},{5,7},{6,8},{7,9},{8,10},{9,11},{10,... | collective-permute-start | bytes 98312 | tf_op jit(solution)/shard_map/ppermute | solution.py:499
  8.7 7.3 %collective-permute-start.3 = (f32[64,128]{1,0:T(8,128)S(1)}, f32[64,128]{1,0:T(8,128)S(1)}, u32[]{:S(2)}, u32[]{:S(2)}) collective-permute-start(f32[64,128]{1,0:T(8,128)S(1)} %get-tuple-element.48), channel_id=1, source_target_pairs={{0,30},{1,31},{2,0},{3,1},{4,2},{5,3},{6,4},{7,5},{8,6},{9,7},{10,... | collective-permute-start | bytes 98312 | tf_op jit(solution)/shard_map/ppermute | solution.py:499
  18.4 7.3 %collective-permute-start.4 = (f32[56,256]{1,0:T(8,128)S(1)}, f32[56,256]{1,0:T(8,128)S(1)}, u32[]{:S(2)}, u32[]{:S(2)}) collective-permute-start(f32[56,256]{1,0:T(8,128)S(1)} %get-tuple-element.64), channel_id=1, source_target_pairs={{0,1},{1,2},{2,3},{3,4},{4,5},{5,6},{6,7},{7,8},{8,9},{9,10},{10,1... | collective-permute-start | bytes 172040 | tf_op jit(solution)/shard_map/ppermute | solution.py:499
  19.7 15.5 %collective-permute-start.5 = (f32[56,256]{1,0:T(8,128)S(1)}, f32[56,256]{1,0:T(8,128)S(1)}, u32[]{:S(2)}, u32[]{:S(2)}) collective-permute-start(f32[56,256]{1,0:T(8,128)S(1)} %get-tuple-element.69), channel_id=1, source_target_pairs={{0,31},{1,0},{2,1},{3,2},{4,3},{5,4},{6,5},{7,6},{8,7},{9,8},{10,9... | collective-permute-start | bytes 172040 | tf_op jit(solution)/shard_map/ppermute | solution.py:499

commit v2 on v1

--- a/solution.py
+++ b/solution.py
@@ -18,6 +18,7 @@
 HALF = 32
 SLAB = 2 * HALF
 THIN = 56
+LIST = 2 * FACE + 1
 FACES = 6
 PENALTY = 80.0
 AXES = ("curve", "group")
@@ -256,8 +257,8 @@
     for side in range(2):
         out = dot_rows(jnp.concatenate(parts_of(traces[side], 2), 0), kept[side])
         ghosts = out[:SLAB] + out[SLAB:]
-        row = lax.broadcasted_iota(jnp.int32, (SLAB, 1), 0)
-        ghosts = jnp.where(row == FACE + 1, lists[side : side + 1] + 1.0, ghosts)
+        row = lax.broadcasted_iota(jnp.int32, (THIN, 1), 0)
+        ghosts = jnp.where(row == LIST, lists[side : side + 1] + 1.0, squeeze(ghosts))
         moving = packed[side * MOVE : (side + 1) * MOVE]
         half = MOVE // 2
         sides.append(jnp.concatenate([ghosts, jnp.concatenate([moving[:half], moving[half:]], 1)], 0))
@@ -355,7 +356,7 @@
     cells = placed_ref.shape[1]
     buffers = (near_up_ref[...], near_down_ref[...])
     records = jnp.concatenate(
-        [piece for buffer in buffers for piece in (buffer[SLAB:, :LANES], buffer[SLAB:, LANES:])], 0
+        [piece for buffer in buffers for piece in (buffer[THIN:, :LANES], buffer[THIN:, LANES:])], 0
     )
     slot = records[:, BLOCK + 1 : BLOCK + 2].astype(jnp.int32) - 1
     slot = jnp.where(slot < 0, -2, slot)
@@ -373,7 +374,7 @@
         slab_ref[face * SLAB : (face + 1) * SLAB] + added[face * SLAB : (face + 1) * SLAB] for face in range(FACES)
     ]
     stiff = stiff_ref[...] + added[FACES * SLAB : FACES * SLAB + ROWS]
-    lists = [buffer[FACE + 1 : FACE + 2] for buffer in buffers]
+    lists = [buffer[LIST : LIST + 1] for buffer in buffers]
     far = jnp.concatenate([far_up_ref[...], far_down_ref[...]], 0)
     moved = [moved_ghosts(some, lists, pair_trace_ref) for some in (packed_ref[...], far)]
     flips = flip_ref[...]
@@ -382,7 +383,7 @@
         chosen = as_bf16(jnp.where(slot == neighbour_ref[face : face + 1], 1.0, 0.0))
         near = beside_ref[face * SLAB : (face + 1) * SLAB] + pick(new_slabs[face ^ 1], chosen, 2)
         if face < 2:
-            ghosts = buffers[face][:SLAB] + (moved[0][face] + moved[1][face])
+            ghosts = spread(buffers[face][:THIN]) + (moved[0][face] + moved[1][face])
             near = near + pick(ghosts, ghost_hot_ref[face], 2)
         jumps = face_jumps(face, near, slabs[face], kappa, neighbour_ref, code_ref, flips)
         terms.append(face_terms(jumps, kappa))
@@ -518,7 +519,7 @@
     big = 2 * ROWS * cells
     near_up, near_down, far_up, far_down, packed, payload, stay, send, nbr, trace_pair = call(
         pack_kernel,
-        [f32(SLAB + MOVE // 2, ghosts)] * 2 + [f32(MOVE, ROWS)] * 2
+        [f32(THIN + MOVE // 2, ghosts)] * 2 + [f32(MOVE, ROWS)] * 2
         + [f32(2 * MOVE, ROWS), whole, i32(1, cells), i32(2, ghosts), i32(FACES, cells), bf16(*trace_pair.shape)],
         [right_side, conductivity[None], destination[None], send_list, trace_pair, neighbour], big * LANES * 6,
         [pltpu.VMEM((BLOCK, cells), jnp.float32), pltpu.VMEM((1, cells), jnp.float32),

time: 36.6 us -> 36.6 us (level)
  no operation moved by 1% of the time
where the time goes in v2:
time: 36.6 us; the launch traced here: 36.4 us
  starting transfers between devices  16.4 us (45%)
  Pallas kernels  9.44 us (26%)
  blocking collectives  9.19 us (25%)
  between operations  0.71 us (2%)
  waiting for transfers between devices  0.62 us (2%)
    ppermute x6, starting transfers between devices, shift(): lax.ppermute(value, AXES, [(i, (i + distance) % count) for i in range(cou...  16.4 us
    pallas_call x6, Pallas kernels, call(): pl.pallas_call(kernel, out_shape=list(outs), in_specs=[pl.BlockSpec(memor...  9.44 us
    all_to_all x1, blocking collectives, body(): sums = lax.all_to_all(sums, AXES, 0, 0, tiled=True)  9.19 us
  transfers between devices with their start and end apart: 6, of which 1 were waited for; matrix products, arithmetic and copies ran while one was open for 0% of the time, Pallas kernels for 12%

profile of v2, /device:TPU:0, one launch (start us, length us, event | category | flops | bytes accessed | tf_op | source)
XLA Modules:
  0.0 36.4 jit_solution(15391368281196304001)
XLA Ops:
  0.6 1.5 %shard_map.131 = (f32[88,256]{1,0:T(8,128)S(1)}, f32[88,256]{1,0:T(8,128)S(1)}, f32[64,128]{1,0:T(8,128)S(1)}, f32[64,128]{1,0:T(8,128)S(1)}, f32[128,128]{1,0:T...) custom-call(f32[125,512]{1,0:T(8,128)} %rhs_hbm.1, ...), custom_call_target="tpu_custom_call" | custom-call | flops 100663296 | bytes 1060864 | tf_op jit(solution)/shard_map/pallas_call | solution.py:183
  2.2 3.0 %collective-permute-start = (f32[88,256]{1,0:T(8,128)S(1)}, f32[88,256]{1,0:T(8,128)S(1)}, u32[]{:S(2)}, u32[]{:S(2)}) collective-permute-start(f32[88,256]{1,0:T(8,128)S(1)} %get-tuple-element.45), channel_id=1, source_target_pairs={{0,1},{1,2},{2,3},{3,4},{4,5},{5,6},{6,7},{7,8},{8,9},{9,10},{10,1... | collective-permute-start | bytes 270344 | tf_op jit(solution)/shard_map/ppermute | solution.py:500
  5.2 3.5 %collective-permute-start.1 = (f32[88,256]{1,0:T(8,128)S(1)}, f32[88,256]{1,0:T(8,128)S(1)}, u32[]{:S(2)}, u32[]{:S(2)}) collective-permute-start(f32[88,256]{1,0:T(8,128)S(1)} %get-tuple-element.46), channel_id=1, source_target_pairs={{0,31},{1,0},{2,1},{3,2},{4,3},{5,4},{6,5},{7,6},{8,7},{9,8},{10,9... | collective-permute-start | bytes 270344 | tf_op jit(solution)/shard_map/ppermute | solution.py:500
  8.7 0.0 collective-permute-start.2
  8.7 4.4 %collective-permute-start.3 = (f32[64,128]{1,0:T(8,128)S(1)}, f32[64,128]{1,0:T(8,128)S(1)}, u32[]{:S(2)}, u32[]{:S(2)}) collective-permute-start(f32[64,128]{1,0:T(8,128)S(1)} %get-tuple-element.48), channel_id=1, source_target_pairs={{0,30},{1,31},{2,0},{3,1},{4,2},{5,3},{6,4},{7,5},{8,6},{9,7},{10,... | collective-permute-start | bytes 98312 | tf_op jit(solution)/shard_map/ppermute | solution.py:500
  13.2 2.8 %shard_map.132 = (f32[128,512]{1,0:T(8,128)S(1)}, bf16[2,512,256]{2,1,0:T(8,128)(2,1)S(1)}, bf16[2,256,512]{2,1,0:T(8,128)(2,1)S(1)}, bf16[6,512,512]{2,1,0:T(8,...) custom-call(s32[6,512]{1,0:T(8,128)} %refs_0_.1, ...), custom_call_target="tpu_custom_call" | custom-call | flops 201326592 | bytes 7939072 | tf_op jit(solution)/shard_map/pallas_call | solution.py:183
  16.0 0.0 collective-permute-done.2.far_up_ref
  16.0 0.0 collective-permute-done.3.far_down_ref
  16.0 0.0 collective-permute-done.near_up_ref
  16.0 0.0 collective-permute-done.1.near_down_ref
  16.0 2.4 %shard_map.133 = (f32[128,512]{1,0:T(8,128)S(1)}, f32[1,512]{1,0:T(1,128)S(1)}, f32[128,512]{1,0:T(8,128)S(1)}, f32[128,512]{1,0:T(8,128)S(1)}, f32[56,256]{1,0:T(8,128)S(1)}) custom-call(f32[128,512]{1,0:T(8,128)S(1)} %get-tuple-element.41.placed_ref, f32[384,512]{1,0:T(8,128)S(1)} %get-tuple-element.42.slab_ref, ...), custom_call_target="tpu_custom_call" | custom-call | flops 805306368 | bytes 5048832 | tf_op jit(solution)/shard_map/pallas_call | solution.py:183
  18.4 0.1 collective-permute-start.4
  18.5 1.2 %shard_map.134 = (f32[128,512]{1,0:T(8,128)S(1)}, f32[128,512]{1,0:T(8,128)S(1)}, f32[1,128]{1,0:T(1,128)S(1)}, f32[56,256]{1,0:T(8,128)S(1)}) custom-call(f32[128,512]{1,0:T(8,128)S(1)} %get-tuple-element.58.image_ref, f32[1,512]{1,0:T(1,128)S(1)} %get-tuple-element.59.kappa_ref, f32[128,512]{1,0:T(8,128)S(1)} %get-tuple-element.60.pair_ref, ...), custom_call_target="tpu_custom_call" | custom-call | flops 805306368 | bytes 5590016 | tf_op jit(solution)/shard_map/pallas_call | solution.py:183
  19.7 5.4 %collective-permute-start.5 = (f32[56,256]{1,0:T(8,128)S(1)}, f32[56,256]{1,0:T(8,128)S(1)}, u32[]{:S(2)}, u32[]{:S(2)}) collective-permute-start(f32[56,256]{1,0:T(8,128)S(1)} %get-tuple-element.69), channel_id=1, source_target_pairs={{0,31},{1,0},{2,1},{3,2},{4,3},{5,4},{6,5},{7,6},{8,7},{9,8},{10,9... | collective-permute-start | bytes 172040 | tf_op jit(solution)/shard_map/ppermute | solution.py:500
  25.1 0.6 %collective-permute-done.4.from_left_ref = f32[56,256]{1,0:T(8,128)S(1)} collective-permute-done((f32[56,256]{1,0:T(8,128)S(1)}, f32[56,256]{1,0:T(8,128)S(1)}, u32[]{:S(2)}, u32[]{:S(2)}) %collective-permute-start.4) | collective-permute-done | bytes 57376 | tf_op jit(solution)/shard_map/ppermute | solution.py:500
  25.7 0.3 shard_map.135
  26.0 9.2 %all_to_all.9 = f32[32,1,128]{2,1,0:T(1,128)S(1)} all-to-all(f32[32,1,128]{2,1,0:T(1,128)S(1)} %bitcast.6), channel_id=1, replica_groups=mesh['curve'=4,'group'=8] {'curve','group'}, dimensions={0} | all-to-all | bytes 32768 | tf_op jit(solution)/shard_map/all_to_all | solution.py:556
  35.2 0.1 reduce_sum.9
  35.2 0.0 collective-permute-done.5.from_right_ref
  35.2 1.2 %shard_map.136 = (f32[125,512]{1,0:T(8,128)}, f32[125,512]{1,0:T(8,128)}) custom-call(f32[1,128]{1,0:T(1,128)S(1)} %bitcast.7, f32[128,512]{1,0:T(8,128)S(1)} %get-tuple-element.62.field_ref, f32[128,512]{1,0:T(8,128)S(1)} %get-tuple-element.58.image_ref, f32[128,512]{1,0:T(8,128)S(1)} %get-tuple-element.67.part_ref, ...), custom_call_target="tpu_custom_call" | custom-call | flops 50331648 | bytes 2693632 | tf_op jit(solution)/shard_map/pallas_call | solution.py:183
Async XLA Ops:
  2.2 13.8 %collective-permute-start = (f32[88,256]{1,0:T(8,128)S(1)}, f32[88,256]{1,0:T(8,128)S(1)}, u32[]{:S(2)}, u32[]{:S(2)}) collective-permute-start(f32[88,256]{1,0:T(8,128)S(1)} %get-tuple-element.45), channel_id=1, source_target_pairs={{0,1},{1,2},{2,3},{3,4},{4,5},{5,6},{6,7},{7,8},{8,9},{9,10},{10,1... | collective-permute-start | bytes 270344 | tf_op jit(solution)/shard_map/ppermute | solution.py:500
  5.2 10.8 %collective-permute-start.1 = (f32[88,256]{1,0:T(8,128)S(1)}, f32[88,256]{1,0:T(8,128)S(1)}, u32[]{:S(2)}, u32[]{:S(2)}) collective-permute-start(f32[88,256]{1,0:T(8,128)S(1)} %get-tuple-element.46), channel_id=1, source_target_pairs={{0,31},{1,0},{2,1},{3,2},{4,3},{5,4},{6,5},{7,6},{8,7},{9,8},{10,9... | collective-permute-start | bytes 270344 | tf_op jit(solution)/shard_map/ppermute | solution.py:500
  8.7 7.3 %collective-permute-start.2 = (f32[64,128]{1,0:T(8,128)S(1)}, f32[64,128]{1,0:T(8,128)S(1)}, u32[]{:S(2)}, u32[]{:S(2)}) collective-permute-start(f32[64,128]{1,0:T(8,128)S(1)} %get-tuple-element.47), channel_id=1, source_target_pairs={{0,2},{1,3},{2,4},{3,5},{4,6},{5,7},{6,8},{7,9},{8,10},{9,11},{10,... | collective-permute-start | bytes 98312 | tf_op jit(solution)/shard_map/ppermute | solution.py:500
  8.7 7.3 %collective-permute-start.3 = (f32[64,128]{1,0:T(8,128)S(1)}, f32[64,128]{1,0:T(8,128)S(1)}, u32[]{:S(2)}, u32[]{:S(2)}) collective-permute-start(f32[64,128]{1,0:T(8,128)S(1)} %get-tuple-element.48), channel_id=1, source_target_pairs={{0,30},{1,31},{2,0},{3,1},{4,2},{5,3},{6,4},{7,5},{8,6},{9,7},{10,... | collective-permute-start | bytes 98312 | tf_op jit(solution)/shard_map/ppermute | solution.py:500
  18.4 7.3 %collective-permute-start.4 = (f32[56,256]{1,0:T(8,128)S(1)}, f32[56,256]{1,0:T(8,128)S(1)}, u32[]{:S(2)}, u32[]{:S(2)}) collective-permute-start(f32[56,256]{1,0:T(8,128)S(1)} %get-tuple-element.64), channel_id=1, source_target_pairs={{0,1},{1,2},{2,3},{3,4},{4,5},{5,6},{6,7},{7,8},{8,9},{9,10},{10,1... | collective-permute-start | bytes 172040 | tf_op jit(solution)/shard_map/ppermute | solution.py:500
  19.7 15.5 %collective-permute-start.5 = (f32[56,256]{1,0:T(8,128)S(1)}, f32[56,256]{1,0:T(8,128)S(1)}, u32[]{:S(2)}, u32[]{:S(2)}) collective-permute-start(f32[56,256]{1,0:T(8,128)S(1)} %get-tuple-element.69), channel_id=1, source_target_pairs={{0,31},{1,0},{2,1},{3,2},{4,3},{5,4},{6,5},{7,6},{8,7},{9,8},{10,9... | collective-permute-start | bytes 172040 | tf_op jit(solution)/shard_map/ppermute | solution.py:500
